TPU v7x, 32 devices: a whole 2x2x4 slice. The times are simulated.
32 devices in a mesh: rep: 2 (over x), fsdp: 4 (over y, core), seq: 4 (over z).
Axes of the slice: x: 2, y: 2, z: 4, core: 2. Of those that a mesh axis runs over, the one named last changes fastest.
Arguments:
- tokens: bfloat16 [16, 1024, 1152], P(('rep', 'fsdp'), 'seq'), may hold values from -6 to 6
- condition: bfloat16 [16, 1152], P(('rep', 'fsdp')), may hold values from -6 to 6
- valid_mask: int32 [16, 1024], P(('rep', 'fsdp'), 'seq'), may hold values from 0 to 1, as said below
- teacher: bfloat16 [16, 1024, 1152], P(('rep', 'fsdp'), 'seq'), may hold values from -6 to 6
- out_grad: bfloat16 [16, 1024, 1152], P(('rep', 'fsdp'), 'seq'), may hold values from -96 to 96
- mod_weight: bfloat16 [1152, 6912], P('fsdp'), may hold values from -0.1875 to 0.1875
- mod_bias: bfloat16 [6912], P('fsdp'), may hold values from -3 to 3
- qkv_weight: bfloat16 [1152, 3456], P('fsdp'), may hold values from -0.1875 to 0.1875
- qkv_bias: bfloat16 [2304], P('fsdp'), may hold values from -3 to 3
- out_weight: bfloat16 [1152, 1152], P('fsdp'), may hold values from -2 to 2
- out_bias: bfloat16 [1152], P('fsdp'), may hold values from -3 to 3
- up_weight: bfloat16 [1152, 4608], P('fsdp'), may hold values from -0.1875 to 0.1875
- up_bias: bfloat16 [4608], P('fsdp'), may hold values from -3 to 3
- down_weight: bfloat16 [4608, 1152], P('fsdp'), may hold values from -0.09375 to 0.09375
- down_bias: bfloat16 [1152], P('fsdp'), may hold values from -3 to 3
Outputs:
- block_out: bfloat16 [16, 1024, 1152], P(('rep', 'fsdp'), 'seq')
- loss_value: float32 [], replicated
- tokens_grad: bfloat16 [16, 1024, 1152], P(('rep', 'fsdp'), 'seq')
- condition_grad: float32 [16, 1152], P(('rep', 'fsdp'))
- mod_weight_grad: float32 [1152, 6912], P('fsdp')
- mod_bias_grad: float32 [6912], P('fsdp')
- qkv_weight_grad: float32 [1152, 3456], P('fsdp')
- qkv_bias_grad: float32 [2304], P('fsdp')
- out_weight_grad: float32 [1152, 1152], P('fsdp')
- out_bias_grad: float32 [1152], P('fsdp')
- up_weight_grad: float32 [1152, 4608], P('fsdp')
- up_bias_grad: float32 [4608], P('fsdp')
- down_weight_grad: float32 [4608, 1152], P('fsdp')
- down_bias_grad: float32 [1152], P('fsdp')
Inputs may be any that keep to these rules, and one draw needn't show every extreme that they name: `valid_mask`: the first token of every latent is valid.
All inputs are finite; a program needn't handle non-finite values.
Results may differ from a plain program's by a relative error of at most 0.012.
Values may be sent and summed in bfloat16 or wider, within the bound.
A program may use at most 256 MiB of HBM per device.

v0:
```python
import jax
import jax.numpy as jnp
from jax import lax
from jax.sharding import PartitionSpec as P

HEADS = 16
EPS = 1e-06
GELU_C = 0.7978845608028654
HIGHEST = lax.Precision.HIGHEST


def norm_rows(inputs):
    centred = inputs - jnp.mean(inputs, axis=-1, keepdims=True)
    return centred * lax.rsqrt(jnp.mean(centred * centred, axis=-1, keepdims=True) + EPS)


def gelu_tanh(inputs):
    return 0.5 * inputs * (1.0 + jnp.tanh(GELU_C * (inputs + 0.044715 * inputs * inputs * inputs)))


def modulate(inputs, offset, stretch):
    return norm_rows(inputs) * (1.0 + stretch) + offset


def flat_dot(left, right):
    return jnp.dot(left.reshape(-1, left.shape[-1]), right, preferred_element_type=jnp.float32)


def flat_dot_t(left, right):
    return lax.dot_general(
        left.reshape(-1, left.shape[-1]),
        right,
        (((1,), (1,)), ((), ())),
        preferred_element_type=jnp.float32,
    )


def outer_sum(left, right):
    return lax.dot_general(
        left.reshape(-1, left.shape[-1]),
        right.reshape(-1, right.shape[-1]),
        (((0,), (0,)), ((), ())),
        preferred_element_type=jnp.float32,
    )


def outer_exact(left, right):
    return lax.dot_general(
        left, right, (((0,), (0,)), ((), ())), precision=HIGHEST, preferred_element_type=jnp.float32
    )


def shards(
    tokens,
    condition,
    valid_mask,
    teacher,
    out_grad,
    mod_weight,
    mod_bias,
    qkv_weight,
    qkv_bias,
    out_weight,
    out_bias,
    up_weight,
    up_bias,
    down_weight,
    down_bias,
):
    gathered = (
        lax.all_gather(mod_weight, "fsdp", axis=0, tiled=True),
        lax.all_gather(mod_bias, "fsdp", axis=0, tiled=True),
        lax.all_gather(qkv_weight, "fsdp", axis=0, tiled=True),
        lax.all_gather(qkv_bias, "fsdp", axis=0, tiled=True),
        lax.all_gather(out_weight, "fsdp", axis=0, tiled=True),
        lax.all_gather(out_bias, "fsdp", axis=0, tiled=True),
        lax.all_gather(up_weight, "fsdp", axis=0, tiled=True),
        lax.all_gather(up_bias, "fsdp", axis=0, tiled=True),
        lax.all_gather(down_weight, "fsdp", axis=0, tiled=True),
        lax.all_gather(down_bias, "fsdp", axis=0, tiled=True),
    )
    (
        mod_full,
        modb_full,
        qkv_full,
        qkvb_full,
        out_full,
        outb_full,
        up_full,
        upb_full,
        down_full,
        downb_full,
    ) = gathered
    latents, rows, width = tokens.shape
    head_dim = width // HEADS
    factor = head_dim ** (-0.5)
    total_tokens = (
        latents * rows * lax.axis_size("rep") * lax.axis_size("fsdp") * lax.axis_size("seq")
    )
    keyvalid = valid_mask.astype(jnp.float32)
    counted = lax.psum(jnp.sum(keyvalid), ("rep", "fsdp", "seq"))
    inputs = tokens.astype(jnp.float32)
    conds = condition.astype(jnp.float32)
    silu_low = jax.nn.silu(conds).astype(jnp.bfloat16)
    modulation = jnp.dot(silu_low, mod_full, preferred_element_type=jnp.float32) + modb_full.astype(
        jnp.float32
    )
    pieces = [modulation[:, None, number * width : (number + 1) * width] for number in range(6)]
    shift_one, scale_one, gate_one, shift_two, scale_two, gate_two = pieces
    hidden_one = modulate(inputs, shift_one, scale_one).astype(jnp.bfloat16)
    projected = flat_dot(hidden_one, qkv_full).reshape(latents, rows, 3 * width)
    qkv_bias_f = qkvb_full.astype(jnp.float32)
    queries = (projected[..., :width] + qkv_bias_f[:width]).astype(jnp.bfloat16)
    keys_own = projected[..., width : 2 * width].astype(jnp.bfloat16)
    values_own = (projected[..., 2 * width :] + qkv_bias_f[width:]).astype(jnp.bfloat16)
    all_keys, all_values, all_valid = (
        lax.all_gather(keys_own, "seq", axis=1, tiled=True),
        lax.all_gather(values_own, "seq", axis=1, tiled=True),
        lax.all_gather(keyvalid.astype(jnp.bfloat16), "seq", axis=1, tiled=True),
    )
    keep_mask = (all_valid > 0.5)[:, None, :]

    def split_heads(tensor):
        return tensor.reshape(latents, tensor.shape[1], HEADS, head_dim).transpose(2, 0, 1, 3)

    def merge_heads(tensor):
        return tensor.transpose(1, 2, 0, 3).reshape(latents, tensor.shape[2], width)

    def scores_of(q_head, k_head, mask):
        scores = (
            jnp.einsum("gqd,gkd->gqk", q_head, k_head, preferred_element_type=jnp.float32) * factor
        )
        return jnp.where(mask, scores, -1e30)

    def head_forward(packed):
        q_head, k_head, v_head = packed
        scores = scores_of(q_head, k_head, keep_mask)
        maxima = jnp.max(scores, axis=-1, keepdims=True)
        expsum = jnp.exp(scores - maxima)
        totals = jnp.sum(expsum, axis=-1, keepdims=True)
        probability = (expsum / totals).astype(jnp.bfloat16)
        mixture = jnp.einsum(
            "gqk,gkd->gqd", probability, v_head, preferred_element_type=jnp.float32
        )
        return (mixture, (maxima + jnp.log(totals))[..., 0])

    q_heads = split_heads(queries)
    k_heads = split_heads(all_keys)
    v_heads = split_heads(all_values)
    mixed_heads, logsum = lax.map(head_forward, (q_heads, k_heads, v_heads))
    attended = merge_heads(mixed_heads).astype(jnp.bfloat16)
    branch = flat_dot(attended, out_full).reshape(latents, rows, width) + outb_full.astype(
        jnp.float32
    )
    middle = inputs + gate_one * branch
    hidden_two = modulate(middle, shift_two, scale_two).astype(jnp.bfloat16)
    up_pre = flat_dot(hidden_two, up_full) + upb_full.astype(jnp.float32)
    activated = gelu_tanh(up_pre).astype(jnp.bfloat16)
    mlp_out = (flat_dot(activated, down_full) + downb_full.astype(jnp.float32)).reshape(
        latents, rows, width
    )
    output = middle + gate_two * mlp_out
    differ = output - teacher.astype(jnp.float32)
    err_sum = jnp.sum(keyvalid[..., None] * differ * differ)
    regathered = (
        lax.all_gather(mod_weight, "fsdp", axis=0, tiled=True),
        lax.all_gather(mod_bias, "fsdp", axis=0, tiled=True),
        lax.all_gather(qkv_weight, "fsdp", axis=0, tiled=True),
        lax.all_gather(qkv_bias, "fsdp", axis=0, tiled=True),
        lax.all_gather(out_weight, "fsdp", axis=0, tiled=True),
        lax.all_gather(out_bias, "fsdp", axis=0, tiled=True),
        lax.all_gather(up_weight, "fsdp", axis=0, tiled=True),
        lax.all_gather(up_bias, "fsdp", axis=0, tiled=True),
        lax.all_gather(down_weight, "fsdp", axis=0, tiled=True),
        lax.all_gather(down_bias, "fsdp", axis=0, tiled=True),
    )
    mod_back = regathered[0]
    qkv_back = regathered[2]
    out_back = regathered[4]
    up_back = regathered[6]
    down_back = regathered[8]
    grad_out = out_grad.astype(jnp.float32) + total_tokens / counted * differ * keyvalid[..., None]
    grad_mlp = (grad_out * gate_two).astype(jnp.bfloat16)
    gate_two_grad = jnp.sum(grad_out * mlp_out, axis=1)
    down_wgrad = outer_sum(activated, grad_mlp)
    down_bgrad = jnp.sum(grad_mlp.astype(jnp.float32), axis=(0, 1))
    act_grad = flat_dot_t(grad_mlp, down_back)
    up_pre_grad = jax.vjp(gelu_tanh, up_pre)[1](act_grad)[0].astype(jnp.bfloat16)
    up_wgrad = outer_sum(hidden_two, up_pre_grad)
    up_bgrad = jnp.sum(up_pre_grad.astype(jnp.float32), axis=0)
    hidden_two_grad = flat_dot_t(up_pre_grad, up_back).reshape(latents, rows, width)
    pull_two = jax.vjp(modulate, middle, shift_two, scale_two)[1]
    middle_part, shift_two_grad, scale_two_grad = pull_two(hidden_two_grad)
    middle_grad = middle_part + grad_out
    branch_grad = (middle_grad * gate_one).astype(jnp.bfloat16)
    gate_one_grad = jnp.sum(middle_grad * branch, axis=1)
    out_wgrad = outer_sum(attended, branch_grad)
    out_bgrad = jnp.sum(branch_grad.astype(jnp.float32), axis=(0, 1))
    attended_grad = (
        flat_dot_t(branch_grad, out_back).astype(jnp.bfloat16).reshape(latents, rows, width)
    )
    dout_heads = split_heads(attended_grad)

    def head_backward(packed):
        q_head, k_head, v_head, lse_head, dout_head = packed
        scores = scores_of(q_head, k_head, keep_mask)
        probability = jnp.exp(scores - lse_head[..., None])
        value_part = jnp.einsum(
            "gqk,gqd->gkd",
            probability.astype(jnp.bfloat16),
            dout_head,
            preferred_element_type=jnp.float32,
        )
        prob_grad = jnp.einsum(
            "gqd,gkd->gqk", dout_head, v_head, preferred_element_type=jnp.float32
        )
        score_grad = (
            probability * (prob_grad - jnp.sum(probability * prob_grad, axis=-1, keepdims=True))
        ).astype(jnp.bfloat16)
        query_part = (
            jnp.einsum("gqk,gkd->gqd", score_grad, k_head, preferred_element_type=jnp.float32)
            * factor
        )
        key_part = (
            jnp.einsum("gqk,gqd->gkd", score_grad, q_head, preferred_element_type=jnp.float32)
            * factor
        )
        return (query_part, key_part, value_part)

    q_grads, k_grads, v_grads = lax.map(
        head_backward, (q_heads, k_heads, v_heads, logsum, dout_heads)
    )
    key_sum, value_sum = (
        lax.psum_scatter(merge_heads(k_grads), "seq", scatter_dimension=1, tiled=True),
        lax.psum_scatter(merge_heads(v_grads), "seq", scatter_dimension=1, tiled=True),
    )
    query_grad = merge_heads(q_grads).astype(jnp.bfloat16)
    value_grad = value_sum.astype(jnp.bfloat16)
    qkv_grad = jnp.concatenate([query_grad, key_sum.astype(jnp.bfloat16), value_grad], axis=-1)
    qkv_wgrad = outer_sum(hidden_one, qkv_grad)
    qkv_bgrad = jnp.concatenate(
        [
            jnp.sum(query_grad.astype(jnp.float32), axis=(0, 1)),
            jnp.sum(value_grad.astype(jnp.float32), axis=(0, 1)),
        ]
    )
    hidden_one_grad = flat_dot_t(qkv_grad, qkv_back).reshape(latents, rows, width)
    pull_one = jax.vjp(modulate, inputs, shift_one, scale_one)[1]
    input_part, shift_one_grad, scale_one_grad = pull_one(hidden_one_grad)
    tokens_grad = (input_part + middle_grad).astype(jnp.bfloat16)
    mod_grad = jnp.concatenate(
        [
            shift_one_grad[:, 0],
            scale_one_grad[:, 0],
            gate_one_grad,
            shift_two_grad[:, 0],
            scale_two_grad[:, 0],
            gate_two_grad,
        ],
        axis=-1,
    )
    cond_total = lax.psum(mod_grad.astype(jnp.bfloat16), "seq").astype(jnp.float32)
    silu_grad = jnp.einsum(
        "le,de->ld", cond_total, mod_back, precision=HIGHEST, preferred_element_type=jnp.float32
    )
    condition_grad = jax.vjp(jax.nn.silu, conds)[1](silu_grad)[0]
    silu_exact = silu_low.astype(jnp.float32)
    mod_term = outer_exact(silu_exact, mod_grad)
    modb_term = jnp.sum(mod_grad, axis=0)
    (
        owned_modw,
        owned_modb,
        owned_qkvw,
        owned_qkvb,
        owned_outw,
        owned_outb,
        owned_upw,
        owned_upb,
        owned_downw,
        owned_downb,
    ) = (
        lax.psum_scatter(
            mod_term.astype(jnp.bfloat16), "fsdp", scatter_dimension=0, tiled=True
        ).astype(jnp.float32),
        lax.psum_scatter(
            modb_term.astype(jnp.bfloat16), "fsdp", scatter_dimension=0, tiled=True
        ).astype(jnp.float32),
        lax.psum_scatter(
            qkv_wgrad.astype(jnp.bfloat16), "fsdp", scatter_dimension=0, tiled=True
        ).astype(jnp.float32),
        lax.psum_scatter(
            qkv_bgrad.astype(jnp.bfloat16), "fsdp", scatter_dimension=0, tiled=True
        ).astype(jnp.float32),
        lax.psum_scatter(
            out_wgrad.astype(jnp.bfloat16), "fsdp", scatter_dimension=0, tiled=True
        ).astype(jnp.float32),
        lax.psum_scatter(
            out_bgrad.astype(jnp.bfloat16), "fsdp", scatter_dimension=0, tiled=True
        ).astype(jnp.float32),
        lax.psum_scatter(
            up_wgrad.astype(jnp.bfloat16), "fsdp", scatter_dimension=0, tiled=True
        ).astype(jnp.float32),
        lax.psum_scatter(
            up_bgrad.astype(jnp.bfloat16), "fsdp", scatter_dimension=0, tiled=True
        ).astype(jnp.float32),
        lax.psum_scatter(
            down_wgrad.astype(jnp.bfloat16), "fsdp", scatter_dimension=0, tiled=True
        ).astype(jnp.float32),
        lax.psum_scatter(
            down_bgrad.astype(jnp.bfloat16), "fsdp", scatter_dimension=0, tiled=True
        ).astype(jnp.float32),
    )
    summed = (
        lax.psum(owned_modw.astype(jnp.bfloat16), ("rep", "seq")).astype(jnp.float32),
        lax.psum(owned_modb.astype(jnp.bfloat16), ("rep", "seq")).astype(jnp.float32),
        lax.psum(owned_qkvw.astype(jnp.bfloat16), ("rep", "seq")).astype(jnp.float32),
        lax.psum(owned_qkvb.astype(jnp.bfloat16), ("rep", "seq")).astype(jnp.float32),
        lax.psum(owned_outw.astype(jnp.bfloat16), ("rep", "seq")).astype(jnp.float32),
        lax.psum(owned_outb.astype(jnp.bfloat16), ("rep", "seq")).astype(jnp.float32),
        lax.psum(owned_upw.astype(jnp.bfloat16), ("rep", "seq")).astype(jnp.float32),
        lax.psum(owned_upb.astype(jnp.bfloat16), ("rep", "seq")).astype(jnp.float32),
        lax.psum(owned_downw.astype(jnp.bfloat16), ("rep", "seq")).astype(jnp.float32),
        lax.psum(owned_downb.astype(jnp.bfloat16), ("rep", "seq")).astype(jnp.float32),
    )
    err_total = lax.psum(err_sum, ("rep", "fsdp", "seq"))
    loss_value = err_total / (width * counted)
    return (
        output.astype(jnp.bfloat16),
        loss_value,
        tokens_grad,
        condition_grad,
        summed[0],
        summed[1],
        summed[2],
        summed[3],
        summed[4],
        summed[5],
        summed[6],
        summed[7],
        summed[8],
        summed[9],
    )


def solution(mesh):
    placed = (
        P(("rep", "fsdp"), "seq", None),
        P(("rep", "fsdp"), None),
        P(("rep", "fsdp"), "seq"),
        P(("rep", "fsdp"), "seq", None),
        P(("rep", "fsdp"), "seq", None),
        P("fsdp", None),
        P("fsdp"),
        P("fsdp", None),
        P("fsdp"),
        P("fsdp", None),
        P("fsdp"),
        P("fsdp", None),
        P("fsdp"),
        P("fsdp", None),
        P("fsdp"),
    )
    return jax.shard_map(
        shards,
        mesh=mesh,
        in_specs=placed,
        out_specs=(
            P(("rep", "fsdp"), "seq", None),
            P(),
            P(("rep", "fsdp"), "seq", None),
            P(("rep", "fsdp"), None),
            P("fsdp", None),
            P("fsdp"),
            P("fsdp", None),
            P("fsdp"),
            P("fsdp", None),
            P("fsdp"),
            P("fsdp", None),
            P("fsdp"),
            P("fsdp", None),
            P("fsdp"),
        ),
        check_vma=False,
    )
```

profile of v0, /device:TPU:0, one launch (start us, length us, event | category | flops | bytes accessed | tf_op | source)
XLA Modules:
  0.0 1927.1 jit_solution(1183738872839530191)
XLA Ops:
  12.4 12.9 all-reduce.13
  26.7 86.8 %all-gather.9.cloned.1.call-done = bf16[1152,6912]{1,0:T(8,128)(2,1)} async-done(((bf16[288,6912]{1,0:T(8,128)(2,1)}), bf16[1152,6912]{1,0:T(8,128)(2,1)}) %all-gather.9.cloned.1.call-update) | async-done | bytes 15925264 | tf_op jit(solution)/shard_map/all_gather | solution.py:71
  113.4 7.7 convolution_add_fusion
  121.8 49.1 %all-gather.11.cloned.1.call-done = bf16[1152,3456]{1,0:T(8,128)(2,1)} async-done(((bf16[288,3456]{1,0:T(8,128)(2,1)}), bf16[1152,3456]{1,0:T(8,128)(2,1)}) %all-gather.11.cloned.1.call-update) | async-done | bytes 7962640 | tf_op jit(solution)/shard_map/all_gather | solution.py:73
  170.9 7.7 fusion.49
  182.0 2.8 slice.65
  188.1 11.4 all_gather.46
  199.5 5.4 all-gather
  208.5 63.0 %all-gather.15.cloned.1.call-done = bf16[2,1024,1152]{2,1,0:T(8,128)(2,1)} async-done(((bf16[2,256,1152]{2,1,0:T(8,128)(2,1)}), bf16[2,1024,1152]{2,1,0:T(8,128)(2,1)}) %all-gather.15.cloned.1.call-update) | async-done | bytes 4718608 | tf_op jit(solution)/shard_map/all_gather | solution.py:118
  271.5 6.6 copy.80
  278.2 5.8 copy.83
  284.0 77.4 %all-gather.13.cloned.1.call-done = bf16[2,1024,1152]{2,1,0:T(8,128)(2,1)} async-done(((bf16[2,256,1152]{2,1,0:T(8,128)(2,1)}), bf16[2,1024,1152]{2,1,0:T(8,128)(2,1)}) %all-gather.13.cloned.1.call-update) | async-done | bytes 4718608 | tf_op jit(solution)/shard_map/all_gather | solution.py:117
  361.4 6.6 copy.79
  368.0 5.8 copy.82
  373.8 71.5 %while.26 = (s32[]{:T(128)}, bf16[16,2,256,72]{2,3,0,1:T(8,128)(2,1)S(1)}, f32[16,2,256]{2,1,0:T(2,128)}, pred[2,1,1024]{2,0,1:T(4,128)(4,1)S(1)}, bf16[16,2,256...) while((s32[]{:T(128)}, ...), condition=%wide.region_5.6_spmd, body=%wide.region_2.5_spmd.sunk | while | flops 157285888 | bytes 7129185 | solution.py:150
  446.4 5.5 fusion.91
  453.4 5.9 all-gather.19.cloned.1.call-done
  459.3 12.8 fusion.96
  472.1 59.7 %all-gather.21.cloned.1.call-done = bf16[4608,1152]{1,0:T(8,128)(2,1)} async-done(((bf16[1152,1152]{1,0:T(8,128)(2,1)}), bf16[4608,1152]{1,0:T(8,128)(2,1)}) %all-gather.21.cloned.1.call-update) | async-done | bytes 10616848 | tf_op jit(solution)/shard_map/all_gather | solution.py:79
  531.8 13.2 convolution_add_fusion.1
  545.0 2.7 fusion.64
  547.8 39.5 %all-reduce.9 = (f32[]{:T(128)}, f32[]{:T(128)}) all-reduce(f32[]{:T(128)} %get-tuple-element.233, f32[]{:T(128)} %convert_reduce_fusion.2), channel_id=1, replica_groups=mesh['rep'=2,'fsdp'=4,'seq'=4] {'rep','fsdp','seq'}, use_global_device_ids=true, to_apply=%region_9.10 | all-reduce | flops 2 | bytes 16 | tf_op jit(solution)/shard_map/psum | solution.py:325
  588.0 3.3 fusion.86
  591.4 18.8 fusion.87
  610.2 10.9 fusion.97
  623.5 3.0 fusion.89
  630.5 142.3 %while.27 = (s32[]{:T(128)}, bf16[16,2,256,72]{2,3,0,1:T(8,128)(2,1)S(1)}, f32[16,2,1024,72]{2,3,0,1:T(8,128)}, f32[16,2,1024,72]{2,3,0,1:T(8,128)}, pred[2,1,10...) while((s32[]{:T(128)}, ...), condition=%wide.region_16.17_spmd, body=%wide.region_14.16_spmd.sunk | while | flops 382389760 | bytes 18398340 | solution.py:230
  772.8 10.0 copy.93
  782.9 10.1 copy.95
  794.6 3.2 fusion.51
  799.1 13.0 convolution_convert_fusion.1
  813.5 10.3 convolution_convert_fusion.2
  824.6 120.6 %reduce-scatter.8.cloned.1.call-done = f32[2,256,1152]{2,1,0:T(8,128)} async-done(((f32[2,1024,1152]{2,1,0:T(8,128)}), f32[2,256,1152]{2,1,0:T(8,128)}) %reduce-scatter.8.cloned.1.call-update) | async-done | bytes 2359312 | tf_op jit(solution)/shard_map/reduce_scatter | solution.py:234
  947.1 162.7 %reduce-scatter.10.cloned.1.call-done = f32[2,256,1152]{2,1,0:T(8,128)} async-done(((f32[2,1024,1152]{2,1,0:T(8,128)}), f32[2,256,1152]{2,1,0:T(8,128)}) %reduce-scatter.10.cloned.1.call-update) | async-done | bytes 2359312 | tf_op jit(solution)/shard_map/reduce_scatter | solution.py:235
  1113.3 7.3 fusion.40
  1125.5 8.5 fusion.63
  1138.5 15.5 convolution_convert_fusion
  1154.1 82.3 %reduce-scatter.20.cloned.1.call-done = bf16[1152,1152]{1,0:T(8,128)(2,1)} async-done(((bf16[4608,1152]{1,0:T(8,128)(2,1)}), bf16[1152,1152]{1,0:T(8,128)(2,1)}) %reduce-scatter.20.cloned.1.call-update) | async-done | bytes 2654224 | tf_op jit(solution)/shard_map/reduce_scatter | solution.py:306
  1236.3 87.7 %reduce-scatter.18.cloned.1.call-done = bf16[288,4608]{1,0:T(8,128)(2,1)} async-done(((bf16[1152,4608]{1,0:T(8,128)(2,1)}), bf16[288,4608]{1,0:T(8,128)(2,1)}) %reduce-scatter.18.cloned.1.call-update) | async-done | bytes 2654224 | tf_op jit(solution)/shard_map/reduce_scatter | solution.py:300
  1324.1 72.1 %reduce-scatter.14.cloned.1.call-done = bf16[288,3456]{1,0:T(8,128)(2,1)} async-done(((bf16[1152,3456]{1,0:T(8,128)(2,1)}), bf16[288,3456]{1,0:T(8,128)(2,1)}) %reduce-scatter.14.cloned.1.call-update) | async-done | bytes 1990672 | tf_op jit(solution)/shard_map/reduce_scatter | solution.py:288
  1396.1 122.6 %reduce-scatter.12.cloned.1.call-done = bf16[288,6912]{1,0:T(8,128)(2,1)} async-done(((bf16[1152,6912]{1,0:T(8,128)(2,1)}), bf16[288,6912]{1,0:T(8,128)(2,1)}) %reduce-scatter.12.cloned.1.call-update) | async-done | bytes 3981328 | tf_op jit(solution)/shard_map/reduce_scatter | solution.py:282
  1526.4 10.9 all-reduce.12
  1537.8 39.9 %all-reduce.10 = (bf16[1728]{0:T(1024)(128)(2,1)S(1)}, bf16[576]{0:T(1024)(128)(2,1)S(1)}, bf16[288]{0:T(512)(128)(2,1)S(1)}, bf16[1152]{0:T(1024)(128)(2,1)S(1)}, bf16[288]{0:T(512)(128)(2,1)S(1)}) all-reduce(bf16[1728]{0:T(1024)(128)(2,1)S(1)} %dynamic-slice.5, ...), channel_id=1, replica_groups=mesh['rep'=2,'fsdp'=4,'seq'=4] {'rep','seq'}, use_global_device_ids=true, to_apply=%region_32.33 | all-reduce | flops 4032 | bytes 16128 | tf_op jit(solution)/shard_map/psum | solution.py:315
  1580.6 17.6 psum.93
  1598.2 10.5 fusion.77
  1608.7 293.2 %all-reduce.16.cloned.1.call-done = (bf16[288,6912]{1,0:T(8,128)(2,1)}, bf16[288,3456]{1,0:T(8,128)(2,1)}, bf16[288,1152]{1,0:T(8,128)(2,1)}, bf16[288,4608]{1,0:T(8,128)(2,1)}, bf16[1152,1152]{1,0:T(8,128)(2,1)}) async-done(((bf16[288,6912]{1,0:T(8,128)(2,1)}, bf16[288,3456]{1,0:T(8,128)(2,1)}, bf16[288,1152]{1,0:T(8,128)(2,1)}, bf16[288,4608]{1,0:T(8,128)(2,1)}, bf16[1152,1152]{1,0:T(8,128)(2,1)}), ...) | async-done | bytes 11943952 | tf_op jit(solution)/shard_map/psum | solution.py:314
  1904.1 6.0 convert_element_type.228
  1913.2 3.0 convert_element_type.240
  (439 shorter events, 271.8 us)
Async XLA Ops:
  7.2 4.4 copy-start.68
  7.2 4.7 copy-start.66
  7.2 4.9 copy-start.63
  7.2 18.1 copy-start
  7.2 106.2 %all-gather.9.cloned.1.call-start = ((), (), s32[]{:S(2)}) async-start(), calls=%async_computation.7 | async-start | bytes 19906560 | tf_op jit(solution)/shard_map/all_gather | solution.py:71
  8.0 105.5 %copy-start.38 = (bf16[2,1152]{1,0:T(2,128)(2,1)S(1)}, bf16[2,1152]{1,0:T(2,128)(2,1)}, u32[]{:S(2)}) copy-start(bf16[2,1152]{1,0:T(2,128)(2,1)} %param.20) | copy-start | bytes 13828
  8.0 162.9 %all-gather.11.cloned.1.call-start = ((), (), s32[]{:S(2)}) async-start(), calls=%async_computation.8 | async-start | bytes 9953280 | tf_op jit(solution)/shard_map/all_gather | solution.py:73
  8.7 262.8 %all-gather.15.cloned.1.call-start = ((), (), s32[]{:S(2)}) async-start(), calls=%async_computation.10 | async-start | bytes 5898240 | tf_op jit(solution)/shard_map/all_gather | solution.py:118
  25.6 145.3 %copy-start.44 = (f32[2,256]{1,0:T(2,128)}, f32[2,256]{1,0:T(2,128)S(1)}, u32[]{:S(2)}) copy-start(f32[2,256]{1,0:T(2,128)S(1)} %broadcast_multiply_fusion.1) | copy-start | bytes 6148
  26.1 144.8 %copy-start.50 = (f32[2,256]{1,0:T(2,128)}, f32[2,256]{1,0:T(2,128)S(1)}, u32[]{:S(2)}) copy-start(f32[2,256]{1,0:T(2,128)S(1)} %fusion.78) | copy-start | bytes 6148
  121.8 56.9 %copy-start.33 = (f32[2,1152]{1,0:T(2,128)}, f32[2,1152]{1,0:T(2,128)S(1)}, u32[]{:S(2)}) copy-start(f32[2,1152]{1,0:T(2,128)S(1)} %get-tuple-element.251) | copy-start | bytes 27652
  121.8 56.9 %copy-start.60 = (f32[2,1152]{1,0:T(2,128)}, f32[2,1152]{1,0:T(2,128)S(1)}, u32[]{:S(2)}) copy-start(f32[2,1152]{1,0:T(2,128)S(1)} %get-tuple-element.250) | copy-start | bytes 27652
  182.0 179.4 %all-gather.13.cloned.1.call-start = ((), (), s32[]{:S(2)}) async-start(), calls=%async_computation.9 | async-start | bytes 5898240 | tf_op jit(solution)/shard_map/all_gather | solution.py:117
  184.9 260.5 %all-gather.17.cloned.1.call-start = ((), (), s32[]{:S(2)}) async-start(), calls=%async_computation.11 | async-start | bytes 3317760 | tf_op jit(solution)/shard_map/all_gather | solution.py:75
  185.5 14.1 copy-start.64
  185.5 273.8 %all-gather.19.cloned.1.call-start = ((), (), s32[]{:S(2)}) async-start(), calls=%async_computation.12 | async-start | bytes 13271040 | tf_op jit(solution)/shard_map/all_gather | solution.py:77
  186.0 345.8 %all-gather.21.cloned.1.call-start = ((), (), s32[]{:S(2)}) async-start(), calls=%async_computation.13 | async-start | bytes 13271040 | tf_op jit(solution)/shard_map/all_gather | solution.py:79
  186.8 758.4 %reduce-scatter.8.cloned.1.call-start = ((), (), s32[]{:S(2)}) async-start(), calls=%async_computation.14 | async-start | bytes 11796480 | tf_op jit(solution)/shard_map/reduce_scatter | solution.py:234
  453.3 6.0 copy-start.24
  472.1 72.9 %copy-start.13 = (bf16[2,256,1152]{2,1,0:T(8,128)(2,1)S(1)}, bf16[2,256,1152]{2,1,0:T(8,128)(2,1)}, u32[]{:S(2)}) copy-start(bf16[2,256,1152]{2,1,0:T(8,128)(2,1)} %param.22) | copy-start | bytes 3538948
  531.8 13.2 copy-start.35
  531.8 13.2 copy-start.57
  591.3 18.8 copy-start.26
  591.4 32.2 %copy-start.3 = (f32[2,256,1152]{2,1,0:T(8,128)}, f32[2,256,1152]{2,1,0:T(8,128)S(1)}, u32[]{:S(2)}) copy-start(f32[2,256,1152]{2,1,0:T(8,128)S(1)} %get-tuple-element.225) | copy-start | bytes 7077892
  610.2 11.0 copy-start.69
  610.2 11.0 copy-start.32
  610.2 11.0 copy-start.37
  772.8 51.0 %copy-start.5 = (bf16[16,2,256,72]{2,3,0,1:T(8,128)(2,1)}, bf16[16,2,256,72]{2,3,0,1:T(8,128)(2,1)S(1)}, u32[]{:S(2)}) copy-start(bf16[16,2,256,72]{2,3,0,1:T(8,128)(2,1)S(1)} %get-tuple-element.108) | copy-start | bytes 3538948
  782.9 326.9 %reduce-scatter.10.cloned.1.call-start = ((), (), s32[]{:S(2)}) async-start(), calls=%async_computation.15 | async-start | bytes 11796480 | tf_op jit(solution)/shard_map/reduce_scatter | solution.py:235
  793.0 361.1 %reduce-scatter.16.cloned.1.call-start = ((), (), s32[]{:S(2)}) async-start(), calls=%async_computation.18 | async-start | bytes 3317760 | tf_op jit(solution)/shard_map/reduce_scatter | solution.py:294
  797.9 438.5 %reduce-scatter.20.cloned.1.call-start = ((), (), s32[]{:S(2)}) async-start(), calls=%async_computation.20 | async-start | bytes 13271040 | tf_op jit(solution)/shard_map/reduce_scatter | solution.py:306
  812.2 511.9 %reduce-scatter.18.cloned.1.call-start = ((), (), s32[]{:S(2)}) async-start(), calls=%async_computation.19 | async-start | bytes 13271040 | tf_op jit(solution)/shard_map/reduce_scatter | solution.py:300
  823.8 572.3 %reduce-scatter.14.cloned.1.call-start = ((), (), s32[]{:S(2)}) async-start(), calls=%async_computation.17 | async-start | bytes 9953280 | tf_op jit(solution)/shard_map/reduce_scatter | solution.py:288
  824.6 287.7 %copy-start.22 = (bf16[2,256,1152]{2,1,0:T(8,128)(2,1)}, bf16[2,256,1152]{2,1,0:T(8,128)(2,1)S(1)}, u32[]{:S(2)}) copy-start(bf16[2,256,1152]{2,1,0:T(8,128)(2,1)S(1)} %copy.96) | copy-start | bytes 3538948
  947.0 173.6 %copy-start.20 = (bf16[2,256,1152]{2,1,0:T(8,128)(2,1)}, bf16[2,256,1152]{2,1,0:T(8,128)(2,1)S(1)}, u32[]{:S(2)}) copy-start(bf16[2,256,1152]{2,1,0:T(8,128)(2,1)S(1)} %convert_element_type.223) | copy-start | bytes 3538948
  947.0 166.3 %copy-start.1 = (bf16[2,256,1152]{2,1,0:T(8,128)(2,1)S(1)}, bf16[2,256,1152]{2,1,0:T(8,128)(2,1)}, u32[]{:S(2)}) copy-start(bf16[2,256,1152]{2,1,0:T(8,128)(2,1)} %param.19) | copy-start | bytes 3538948
  947.0 166.3 %copy-start.34 = (f32[2,1152]{1,0:T(2,128)S(1)}, f32[2,1152]{1,0:T(2,128)}, u32[]{:S(2)}) copy-start(f32[2,1152]{1,0:T(2,128)} %copy-done.33) | copy-start | bytes 27652
  947.0 166.3 %copy-start.45 = (f32[2,256]{1,0:T(2,128)S(1)}, f32[2,256]{1,0:T(2,128)}, u32[]{:S(2)}) copy-start(f32[2,256]{1,0:T(2,128)} %copy-done.44) | copy-start | bytes 6148
  1120.6 398.1 %reduce-scatter.12.cloned.1.call-start = ((), (), s32[]{:S(2)}) async-start(), calls=%async_computation.16 | async-start | bytes 19906560 | tf_op jit(solution)/shard_map/reduce_scatter | solution.py:282
  1125.5 8.5 copy-start.54
  1125.5 8.5 copy-start.52
  1125.5 9.8 copy-start.9
  1154.0 747.8 %all-reduce.16.cloned.1.call-start = ((), (), s32[]{:S(2)}) async-start(), calls=%async_computation.21 | async-start | bytes 23887872 | tf_op jit(solution)/shard_map/psum | solution.py:314
  1518.7 4.9 copy-start.6
  1521.7 4.6 copy-start.58
  1521.8 4.6 copy-start.59
  1521.8 76.4 %copy-start.40 = (bf16[2,1152]{1,0:T(2,128)(2,1)S(1)}, bf16[2,1152]{1,0:T(2,128)(2,1)}, u32[]{:S(2)}) copy-start(bf16[2,1152]{1,0:T(2,128)(2,1)} %param.20) | copy-start | bytes 13828
  1904.1 6.0 copy-start.17
  (37 other events, 71.5 us)
Sparse Core Ops, SparseCore 0:
  9.6 103.7 all-gather.8
  115.0 55.8 all-gather.10
  182.1 89.3 all-gather.14
  273.5 87.7 all-gather.12
  362.8 24.1 all-gather.16
  388.4 70.9 all-gather.18
  460.9 70.9 all-gather.20
  783.0 162.1 reduce-scatter.7
  947.6 162.1 reduce-scatter.9
  1112.8 35.6 reduce-scatter.15
  1151.1 85.2 reduce-scatter.19
  1238.8 85.2 reduce-scatter.17
  1327.2 68.8 reduce-scatter.13
  1398.6 120.0 reduce-scatter.11
  1523.7 378.1 all-reduce.15
where the time goes:
time: 1940 us; the launch traced here: 1930 us
  waiting for transfers between devices  1290 us (66%)
  matrix products  325 us (17%)
  blocking collectives  138 us (7%)
  local copies, waits for them, and re-layouts  80.1 us (4%)
  other arithmetic  72.8 us (4%)
  between operations  23.3 us (1%)
    psum x1, waiting for transfers between devices, shards(): lax.psum(owned_modw.astype(jnp.bfloat16), ('rep', 'seq'))  293 us
    reduce_scatter x1, waiting for transfers between devices, shards(): lax.psum_scatter(merge_heads(v_grads), 'seq', scatter_dimension=1, tiled=...  163 us
    reduce_scatter x1, waiting for transfers between devices, shards(): lax.psum_scatter(mod_term.astype(jnp.bfloat16), 'fsdp', scatter_dimension...  123 us
    reduce_scatter x1, waiting for transfers between devices, shards(): lax.psum_scatter(merge_heads(k_grads), 'seq', scatter_dimension=1, tiled=...  121 us
    reduce_scatter x1, waiting for transfers between devices, shards(): lax.psum_scatter(up_wgrad.astype(jnp.bfloat16), 'fsdp', scatter_dimension...  87.7 us
    all_gather x1, waiting for transfers between devices, shards(): lax.all_gather(mod_weight, 'fsdp', axis=0, tiled=True)  86.8 us
    reduce_scatter x1, waiting for transfers between devices, shards(): lax.psum_scatter(down_wgrad.astype(jnp.bfloat16), 'fsdp', scatter_dimensi...  82.3 us
    all_gather x1, waiting for transfers between devices, shards(): lax.all_gather(keys_own, 'seq', axis=1, tiled=True)  77.4 us
  transfers between devices with their start and end apart: 15, of which 13 were waited for; matrix products, arithmetic and copies ran while one was open for 12% of the time, Pallas kernels for 0%

commit v1 on v0

--- a/solution.py
+++ b/solution.py
@@ -311,7 +311,9 @@
         ).astype(jnp.float32),
     )
     summed = (
-        lax.psum(owned_modw.astype(jnp.bfloat16), ("rep", "seq")).astype(jnp.float32),
+        jnp.sum(lax.all_gather(owned_modw.astype(jnp.bfloat16), ("rep", "seq")), axis=0).astype(
+            jnp.float32
+        ),
         lax.psum(owned_modb.astype(jnp.bfloat16), ("rep", "seq")).astype(jnp.float32),
         lax.psum(owned_qkvw.astype(jnp.bfloat16), ("rep", "seq")).astype(jnp.float32),
         lax.psum(owned_qkvb.astype(jnp.bfloat16), ("rep", "seq")).astype(jnp.float32),

time: 1940 us -> 2430 us (1.25)
  waiting for transfers between devices: 1290 us -> 1760 us
    all_gather x0 -> x1, waiting for transfers between devices: none -> 595 us  [shards(): lax.all_gather(owned_modw.astype(jnp.bfloat16), ('rep', 'seq'))]
    psum x1, waiting for transfers between devices: 293 us -> 174 us  [shards(): lax.psum(owned_qkvw.astype(jnp.bfloat16), ('rep', 'seq'))]
  transfers between devices with their start and end apart: 15 -> 16, of which waited for: 13 -> 14; matrix products, arithmetic and copies ran while one was open for 12% -> 10% of each run, Pallas kernels for 0% -> 0%
where the time goes in v1:
time: 2430 us; the launch traced here: 2420 us
  waiting for transfers between devices  1760 us (72%)
  matrix products  325 us (13%)
  blocking collectives  138 us (6%)
  other arithmetic  86.5 us (4%)
  local copies, waits for them, and re-layouts  80.1 us (3%)
    all_gather x1, waiting for transfers between devices, shards(): lax.all_gather(owned_modw.astype(jnp.bfloat16), ('rep', 'seq'))  595 us
    psum x1, waiting for transfers between devices, shards(): lax.psum(owned_qkvw.astype(jnp.bfloat16), ('rep', 'seq'))  174 us
    reduce_scatter x1, waiting for transfers between devices, shards(): lax.psum_scatter(merge_heads(v_grads), 'seq', scatter_dimension=1, tiled=...  163 us
    reduce_scatter x1, waiting for transfers between devices, shards(): lax.psum_scatter(mod_term.astype(jnp.bfloat16), 'fsdp', scatter_dimension...  122 us
    reduce_scatter x1, waiting for transfers between devices, shards(): lax.psum_scatter(merge_heads(k_grads), 'seq', scatter_dimension=1, tiled=...  121 us
    reduce_scatter x1, waiting for transfers between devices, shards(): lax.psum_scatter(up_wgrad.astype(jnp.bfloat16), 'fsdp', scatter_dimension...  87.7 us
    all_gather x1, waiting for transfers between devices, shards(): lax.all_gather(mod_weight, 'fsdp', axis=0, tiled=True)  86.8 us
    reduce_scatter x1, waiting for transfers between devices, shards(): lax.psum_scatter(down_wgrad.astype(jnp.bfloat16), 'fsdp', scatter_dimensi...  82.2 us
  transfers between devices with their start and end apart: 16, of which 14 were waited for; matrix products, arithmetic and copies ran while one was open for 10% of the time, Pallas kernels for 0%

profile of v1, /device:TPU:0, one launch (start us, length us, event | category | flops | bytes accessed | tf_op | source)
XLA Modules:
  0.0 2416.8 jit_solution(16451416415060393768)
XLA Ops:
  12.4 12.9 all-reduce.13
  26.7 86.8 %all-gather.11.cloned.1.call-done = bf16[1152,6912]{1,0:T(8,128)(2,1)} async-done(((bf16[288,6912]{1,0:T(8,128)(2,1)}), bf16[1152,6912]{1,0:T(8,128)(2,1)}) %all-gather.11.cloned.1.call-update) | async-done | bytes 15925264 | tf_op jit(solution)/shard_map/all_gather | solution.py:71
  113.4 7.7 convolution_add_fusion
  121.8 49.1 %all-gather.13.cloned.1.call-done = bf16[1152,3456]{1,0:T(8,128)(2,1)} async-done(((bf16[288,3456]{1,0:T(8,128)(2,1)}), bf16[1152,3456]{1,0:T(8,128)(2,1)}) %all-gather.13.cloned.1.call-update) | async-done | bytes 7962640 | tf_op jit(solution)/shard_map/all_gather | solution.py:73
  170.9 7.7 fusion.49
  188.1 11.4 all_gather.52
  199.5 5.4 all-gather.1
  208.5 63.0 %all-gather.17.cloned.1.call-done = bf16[2,1024,1152]{2,1,0:T(8,128)(2,1)} async-done(((bf16[2,256,1152]{2,1,0:T(8,128)(2,1)}), bf16[2,1024,1152]{2,1,0:T(8,128)(2,1)}) %all-gather.17.cloned.1.call-update) | async-done | bytes 4718608 | tf_op jit(solution)/shard_map/all_gather | solution.py:118
  271.5 6.6 copy.80
  278.2 5.8 copy.83
  284.0 77.4 %all-gather.15.cloned.1.call-done = bf16[2,1024,1152]{2,1,0:T(8,128)(2,1)} async-done(((bf16[2,256,1152]{2,1,0:T(8,128)(2,1)}), bf16[2,1024,1152]{2,1,0:T(8,128)(2,1)}) %all-gather.15.cloned.1.call-update) | async-done | bytes 4718608 | tf_op jit(solution)/shard_map/all_gather | solution.py:117
  361.4 6.6 copy.79
  368.0 5.8 copy.82
  373.8 71.5 %while.26 = (s32[]{:T(128)}, bf16[16,2,256,72]{2,3,0,1:T(8,128)(2,1)S(1)}, f32[16,2,256]{2,1,0:T(2,128)}, pred[2,1,1024]{2,0,1:T(4,128)(4,1)S(1)}, bf16[16,2,256...) while((s32[]{:T(128)}, ...), condition=%wide.region_5.6_spmd, body=%wide.region_2.5_spmd.sunk | while | flops 157285888 | bytes 7129185 | solution.py:150
  446.4 5.5 fusion.91
  453.4 5.9 all-gather.21.cloned.1.call-done
  459.3 12.8 fusion.96
  472.1 59.7 %all-gather.23.cloned.1.call-done = bf16[4608,1152]{1,0:T(8,128)(2,1)} async-done(((bf16[1152,1152]{1,0:T(8,128)(2,1)}), bf16[4608,1152]{1,0:T(8,128)(2,1)}) %all-gather.23.cloned.1.call-update) | async-done | bytes 10616848 | tf_op jit(solution)/shard_map/all_gather | solution.py:79
  531.8 13.2 convolution_add_fusion.1
  547.8 39.5 %all-reduce.9 = (f32[]{:T(128)}, f32[]{:T(128)}) all-reduce(f32[]{:T(128)} %get-tuple-element.232, f32[]{:T(128)} %convert_reduce_fusion.2), channel_id=1, replica_groups=mesh['rep'=2,'fsdp'=4,'seq'=4] {'rep','fsdp','seq'}, use_global_device_ids=true, to_apply=%region_9.10 | all-reduce | flops 2 | bytes 16 | tf_op jit(solution)/shard_map/psum | solution.py:327
  588.0 3.3 fusion.86
  591.4 18.8 fusion.87
  610.2 10.9 fusion.97
  623.5 3.0 fusion.89
  630.5 142.3 %while.27 = (s32[]{:T(128)}, bf16[16,2,256,72]{2,3,0,1:T(8,128)(2,1)S(1)}, f32[16,2,1024,72]{2,3,0,1:T(8,128)}, f32[16,2,1024,72]{2,3,0,1:T(8,128)}, pred[2,1,10...) while((s32[]{:T(128)}, ...), condition=%wide.region_16.17_spmd, body=%wide.region_14.16_spmd.sunk | while | flops 382389760 | bytes 18398340 | solution.py:230
  772.8 10.0 copy.93
  782.9 10.1 copy.95
  794.6 3.2 fusion.51
  799.1 13.0 convolution_convert_fusion.1
  813.4 10.3 convolution_convert_fusion.2
  824.6 120.7 %reduce-scatter.8.cloned.1.call-done = f32[2,256,1152]{2,1,0:T(8,128)} async-done(((f32[2,1024,1152]{2,1,0:T(8,128)}), f32[2,256,1152]{2,1,0:T(8,128)}) %reduce-scatter.8.cloned.1.call-update) | async-done | bytes 2359312 | tf_op jit(solution)/shard_map/reduce_scatter | solution.py:234
  947.1 162.7 %reduce-scatter.10.cloned.1.call-done = f32[2,256,1152]{2,1,0:T(8,128)} async-done(((f32[2,1024,1152]{2,1,0:T(8,128)}), f32[2,256,1152]{2,1,0:T(8,128)}) %reduce-scatter.10.cloned.1.call-update) | async-done | bytes 2359312 | tf_op jit(solution)/shard_map/reduce_scatter | solution.py:235
  1113.3 7.3 fusion.40
  1125.5 8.5 fusion.63
  1138.5 15.5 convolution_convert_fusion
  1154.1 82.2 %reduce-scatter.20.cloned.1.call-done = bf16[1152,1152]{1,0:T(8,128)(2,1)} async-done(((bf16[4608,1152]{1,0:T(8,128)(2,1)}), bf16[1152,1152]{1,0:T(8,128)(2,1)}) %reduce-scatter.20.cloned.1.call-update) | async-done | bytes 2654224 | tf_op jit(solution)/shard_map/reduce_scatter | solution.py:306
  1236.3 87.7 %reduce-scatter.18.cloned.1.call-done = bf16[288,4608]{1,0:T(8,128)(2,1)} async-done(((bf16[1152,4608]{1,0:T(8,128)(2,1)}), bf16[288,4608]{1,0:T(8,128)(2,1)}) %reduce-scatter.18.cloned.1.call-update) | async-done | bytes 2654224 | tf_op jit(solution)/shard_map/reduce_scatter | solution.py:300
  1324.1 72.1 %reduce-scatter.14.cloned.1.call-done = bf16[288,3456]{1,0:T(8,128)(2,1)} async-done(((bf16[1152,3456]{1,0:T(8,128)(2,1)}), bf16[288,3456]{1,0:T(8,128)(2,1)}) %reduce-scatter.14.cloned.1.call-update) | async-done | bytes 1990672 | tf_op jit(solution)/shard_map/reduce_scatter | solution.py:288
  1396.2 122.5 %reduce-scatter.12.cloned.1.call-done = bf16[288,6912]{1,0:T(8,128)(2,1)} async-done(((bf16[1152,6912]{1,0:T(8,128)(2,1)}), bf16[288,6912]{1,0:T(8,128)(2,1)}) %reduce-scatter.12.cloned.1.call-update) | async-done | bytes 3981328 | tf_op jit(solution)/shard_map/reduce_scatter | solution.py:282
  1526.1 10.9 all-reduce.12
  1537.4 40.0 %all-reduce.10 = (bf16[1728]{0:T(1024)(128)(2,1)S(1)}, bf16[576]{0:T(1024)(128)(2,1)S(1)}, bf16[288]{0:T(512)(128)(2,1)S(1)}, bf16[1152]{0:T(1024)(128)(2,1)S(1)}, bf16[288]{0:T(512)(128)(2,1)S(1)}) all-reduce(bf16[1728]{0:T(1024)(128)(2,1)S(1)} %dynamic-slice.5, ...), channel_id=1, replica_groups=mesh['rep'=2,'fsdp'=4,'seq'=4] {'rep','seq'}, use_global_device_ids=true, to_apply=%region_32.33 | all-reduce | flops 4032 | bytes 16128 | tf_op jit(solution)/shard_map/psum | solution.py:317
  1580.4 17.7 psum.86
  1598.1 10.5 fusion.77
  1608.6 174.3 %all-reduce.16.cloned.1.call-done = (bf16[288,3456]{1,0:T(8,128)(2,1)}, bf16[288,1152]{1,0:T(8,128)(2,1)}, bf16[288,4608]{1,0:T(8,128)(2,1)}, bf16[1152,1152]{1,0:T(8,128)(2,1)}) async-done(((bf16[288,3456]{1,0:T(8,128)(2,1)}, bf16[288,1152]{1,0:T(8,128)(2,1)}, bf16[288,4608]{1,0:T(8,128)(2,1)}, bf16[1152,1152]{1,0:T(8,128)(2,1)}), (bf16[288,3456]{1,0:T(8,128)(2,1)}, bf16[288,1152]{1,0:T(8,128)(2,1)}, ...) | async-done | bytes 7962640 | tf_op jit(solution)/shard_map/psum | solution.py:318
  1788.4 3.1 convert_element_type.242
  1794.3 594.9 %all-gather.25.cloned.1.call-done = bf16[2304,6912]{1,0:T(8,128)(2,1)} async-done(((bf16[288,6912]{1,0:T(8,128)(2,1)}), bf16[2304,6912]{1,0:T(8,128)(2,1)}) %all-gather.25.cloned.1.call-update) | async-done | bytes 31850512 | tf_op jit(solution)/shard_map/all_gather | solution.py:314
  2389.2 13.6 reduce_sum.287
  2402.7 5.9 convert_element_type.230
  (443 shorter events, 277.6 us)
Async XLA Ops:
  7.2 4.7 copy-start.66
  7.2 4.9 copy-start.63
  7.2 18.1 copy-start
  7.2 106.2 %all-gather.11.cloned.1.call-start = ((), (), s32[]{:S(2)}) async-start(), calls=%async_computation.7 | async-start | bytes 19906560 | tf_op jit(solution)/shard_map/all_gather | solution.py:71
  8.0 105.5 %copy-start.38 = (bf16[2,1152]{1,0:T(2,128)(2,1)S(1)}, bf16[2,1152]{1,0:T(2,128)(2,1)}, u32[]{:S(2)}) copy-start(bf16[2,1152]{1,0:T(2,128)(2,1)} %param.20) | copy-start | bytes 13828
  8.0 162.9 %all-gather.13.cloned.1.call-start = ((), (), s32[]{:S(2)}) async-start(), calls=%async_computation.8 | async-start | bytes 9953280 | tf_op jit(solution)/shard_map/all_gather | solution.py:73
  8.7 262.8 %all-gather.17.cloned.1.call-start = ((), (), s32[]{:S(2)}) async-start(), calls=%async_computation.10 | async-start | bytes 5898240 | tf_op jit(solution)/shard_map/all_gather | solution.py:118
  25.6 145.3 %copy-start.44 = (f32[2,256]{1,0:T(2,128)}, f32[2,256]{1,0:T(2,128)S(1)}, u32[]{:S(2)}) copy-start(f32[2,256]{1,0:T(2,128)S(1)} %broadcast_multiply_fusion.1) | copy-start | bytes 6148
  26.1 144.8 %copy-start.50 = (f32[2,256]{1,0:T(2,128)}, f32[2,256]{1,0:T(2,128)S(1)}, u32[]{:S(2)}) copy-start(f32[2,256]{1,0:T(2,128)S(1)} %fusion.78) | copy-start | bytes 6148
  121.8 56.9 %copy-start.33 = (f32[2,1152]{1,0:T(2,128)}, f32[2,1152]{1,0:T(2,128)S(1)}, u32[]{:S(2)}) copy-start(f32[2,1152]{1,0:T(2,128)S(1)} %get-tuple-element.250) | copy-start | bytes 27652
  121.8 56.9 %copy-start.60 = (f32[2,1152]{1,0:T(2,128)}, f32[2,1152]{1,0:T(2,128)S(1)}, u32[]{:S(2)}) copy-start(f32[2,1152]{1,0:T(2,128)S(1)} %get-tuple-element.249) | copy-start | bytes 27652
  182.0 179.4 %all-gather.15.cloned.1.call-start = ((), (), s32[]{:S(2)}) async-start(), calls=%async_computation.9 | async-start | bytes 5898240 | tf_op jit(solution)/shard_map/all_gather | solution.py:117
  184.9 260.5 %all-gather.19.cloned.1.call-start = ((), (), s32[]{:S(2)}) async-start(), calls=%async_computation.11 | async-start | bytes 3317760 | tf_op jit(solution)/shard_map/all_gather | solution.py:75
  185.5 14.1 copy-start.64
  185.5 273.8 %all-gather.21.cloned.1.call-start = ((), (), s32[]{:S(2)}) async-start(), calls=%async_computation.12 | async-start | bytes 13271040 | tf_op jit(solution)/shard_map/all_gather | solution.py:77
  186.0 345.8 %all-gather.23.cloned.1.call-start = ((), (), s32[]{:S(2)}) async-start(), calls=%async_computation.13 | async-start | bytes 13271040 | tf_op jit(solution)/shard_map/all_gather | solution.py:79
  186.8 758.4 %reduce-scatter.8.cloned.1.call-start = ((), (), s32[]{:S(2)}) async-start(), calls=%async_computation.14 | async-start | bytes 11796480 | tf_op jit(solution)/shard_map/reduce_scatter | solution.py:234
  453.3 6.0 copy-start.24
  472.1 72.9 %copy-start.13 = (bf16[2,256,1152]{2,1,0:T(8,128)(2,1)S(1)}, bf16[2,256,1152]{2,1,0:T(8,128)(2,1)}, u32[]{:S(2)}) copy-start(bf16[2,256,1152]{2,1,0:T(8,128)(2,1)} %param.22) | copy-start | bytes 3538948
  531.8 13.2 copy-start.35
  531.8 13.2 copy-start.57
  591.3 18.8 copy-start.26
  591.3 32.2 %copy-start.3 = (f32[2,256,1152]{2,1,0:T(8,128)}, f32[2,256,1152]{2,1,0:T(8,128)S(1)}, u32[]{:S(2)}) copy-start(f32[2,256,1152]{2,1,0:T(8,128)S(1)} %get-tuple-element.224) | copy-start | bytes 7077892
  610.2 11.0 copy-start.69
  610.2 11.0 copy-start.32
  610.2 11.0 copy-start.37
  772.8 51.0 %copy-start.5 = (bf16[16,2,256,72]{2,3,0,1:T(8,128)(2,1)}, bf16[16,2,256,72]{2,3,0,1:T(8,128)(2,1)S(1)}, u32[]{:S(2)}) copy-start(bf16[16,2,256,72]{2,3,0,1:T(8,128)(2,1)S(1)} %get-tuple-element.108) | copy-start | bytes 3538948
  782.9 326.9 %reduce-scatter.10.cloned.1.call-start = ((), (), s32[]{:S(2)}) async-start(), calls=%async_computation.15 | async-start | bytes 11796480 | tf_op jit(solution)/shard_map/reduce_scatter | solution.py:235
  793.0 361.1 %reduce-scatter.16.cloned.1.call-start = ((), (), s32[]{:S(2)}) async-start(), calls=%async_computation.18 | async-start | bytes 3317760 | tf_op jit(solution)/shard_map/reduce_scatter | solution.py:294
  797.8 438.5 %reduce-scatter.20.cloned.1.call-start = ((), (), s32[]{:S(2)}) async-start(), calls=%async_computation.20 | async-start | bytes 13271040 | tf_op jit(solution)/shard_map/reduce_scatter | solution.py:306
  812.1 511.9 %reduce-scatter.18.cloned.1.call-start = ((), (), s32[]{:S(2)}) async-start(), calls=%async_computation.19 | async-start | bytes 13271040 | tf_op jit(solution)/shard_map/reduce_scatter | solution.py:300
  823.8 572.4 %reduce-scatter.14.cloned.1.call-start = ((), (), s32[]{:S(2)}) async-start(), calls=%async_computation.17 | async-start | bytes 9953280 | tf_op jit(solution)/shard_map/reduce_scatter | solution.py:288
  824.5 287.7 %copy-start.22 = (bf16[2,256,1152]{2,1,0:T(8,128)(2,1)}, bf16[2,256,1152]{2,1,0:T(8,128)(2,1)S(1)}, u32[]{:S(2)}) copy-start(bf16[2,256,1152]{2,1,0:T(8,128)(2,1)S(1)} %copy.96) | copy-start | bytes 3538948
  947.0 173.6 %copy-start.20 = (bf16[2,256,1152]{2,1,0:T(8,128)(2,1)}, bf16[2,256,1152]{2,1,0:T(8,128)(2,1)S(1)}, u32[]{:S(2)}) copy-start(bf16[2,256,1152]{2,1,0:T(8,128)(2,1)S(1)} %convert_element_type.225) | copy-start | bytes 3538948
  947.0 166.3 %copy-start.1 = (bf16[2,256,1152]{2,1,0:T(8,128)(2,1)S(1)}, bf16[2,256,1152]{2,1,0:T(8,128)(2,1)}, u32[]{:S(2)}) copy-start(bf16[2,256,1152]{2,1,0:T(8,128)(2,1)} %param.19) | copy-start | bytes 3538948
  947.1 166.2 %copy-start.34 = (f32[2,1152]{1,0:T(2,128)S(1)}, f32[2,1152]{1,0:T(2,128)}, u32[]{:S(2)}) copy-start(f32[2,1152]{1,0:T(2,128)} %copy-done.33) | copy-start | bytes 27652
  947.1 166.2 %copy-start.45 = (f32[2,256]{1,0:T(2,128)S(1)}, f32[2,256]{1,0:T(2,128)}, u32[]{:S(2)}) copy-start(f32[2,256]{1,0:T(2,128)} %copy-done.44) | copy-start | bytes 6148
  1120.6 398.1 %reduce-scatter.12.cloned.1.call-start = ((), (), s32[]{:S(2)}) async-start(), calls=%async_computation.16 | async-start | bytes 19906560 | tf_op jit(solution)/shard_map/reduce_scatter | solution.py:282
  1125.5 8.5 copy-start.54
  1125.5 8.5 copy-start.52
  1125.5 9.8 copy-start.9
  1154.0 628.9 %all-reduce.16.cloned.1.call-start = ((), (), s32[]{:S(2)}) async-start(), calls=%async_computation.22 | async-start | bytes 15925248 | tf_op jit(solution)/shard_map/psum | solution.py:318
  1396.2 125.3 %copy-start.2 = (f32[2,256,1152]{2,1,0:T(8,128)S(1)}, f32[2,256,1152]{2,1,0:T(8,128)}, u32[]{:S(2)}) copy-start(f32[2,256,1152]{2,1,0:T(8,128)} %get-tuple-element.233) | copy-start | bytes 7077892
  1396.2 993.0 %all-gather.25.cloned.1.call-start = ((), (), s32[]{:S(2)}) async-start(), calls=%async_computation.21 | async-start | bytes 35831808 | tf_op jit(solution)/shard_map/all_gather | solution.py:314
  1518.7 4.6 copy-start.6
  1521.4 4.6 copy-start.58
  1521.4 4.6 copy-start.59
  1521.5 76.7 %copy-start.40 = (bf16[2,1152]{1,0:T(2,128)(2,1)S(1)}, bf16[2,1152]{1,0:T(2,128)(2,1)}, u32[]{:S(2)}) copy-start(bf16[2,1152]{1,0:T(2,128)(2,1)} %param.20) | copy-start | bytes 13828
  (38 other events, 75.4 us)
Sparse Core Ops, SparseCore 0:
  9.6 103.7 all-gather.10
  115.0 55.8 all-gather.12
  182.1 89.3 all-gather.16
  273.5 87.7 all-gather.14
  362.8 24.1 all-gather.18
  388.4 70.9 all-gather.20
  460.9 70.9 all-gather.22
  783.0 162.2 reduce-scatter.7
  947.6 162.1 reduce-scatter.9
  1112.8 35.7 reduce-scatter.15
  1151.1 85.1 reduce-scatter.19
  1238.8 85.2 reduce-scatter.17
  1327.2 68.8 reduce-scatter.13
  1398.6 120.0 reduce-scatter.11
  1523.0 259.9 all-reduce.15
  1784.3 604.7 all-gather.24
